TPU v7x, 32 devices: a whole 2x2x4 slice. The times are simulated.
32 devices in a mesh: expert: 4 (over y, core), unit: 8 (over z, x).
Axes of the slice: x: 2, y: 2, z: 4, core: 2. Of those that a mesh axis runs over, the one named last changes fastest.
Arguments:
- a_gate: bfloat16 [4, 14336, 4096], P('expert', 'unit'), may hold values from -0.09375 to 0.09375
- a_up: bfloat16 [4, 14336, 4096], P('expert', 'unit'), may hold values from -0.09375 to 0.09375
- b_gate: bfloat16 [4, 14336, 4096], P('expert', 'unit'), may hold values from -0.09375 to 0.09375
- b_up: bfloat16 [4, 14336, 4096], P('expert', 'unit'), may hold values from -0.09375 to 0.09375
- order: int32 [4, 448], P('expert'), may hold values from 0 to 447, each once within a row
- calib: bfloat16 [128, 4096], P(('expert', 'unit')), may hold values from -6 to 6
Outputs:
- merged_gate: bfloat16 [4, 14336, 4096], P('expert', 'unit')
- merged_up: bfloat16 [4, 14336, 4096], P('expert', 'unit')
- hidden: bfloat16 [4, 14336, 128], P('expert', 'unit')
Inputs may be any that keep to these rules, and one draw needn't show every extreme that they name: Each row of order is a permutation of the 448 block numbers.
All inputs are finite; a program needn't handle non-finite values.
Results may differ from a plain program's by a relative error of at most 0.006.
Values may be sent and summed in bfloat16 or wider, within the bound.
A program may use at most 256 MiB of HBM per device.

v0:
```python
import jax
import jax.numpy as jnp
from jax import lax
from jax.sharding import PartitionSpec as P

BLOCK = 32


def average(first, second):
    return ((first.astype(jnp.float32) + second.astype(jnp.float32)) * 0.5).astype(jnp.bfloat16)


def local(a_gate, a_up, b_gate, b_up, order, calib):
    blocks = order.shape[1]
    total = blocks * BLOCK
    inverse = jnp.zeros((blocks,), jnp.int32).at[order[0]].set(jnp.arange(blocks, dtype=jnp.int32))

    def relocate(columns):
        grouped = columns.reshape(blocks, BLOCK, columns.shape[1])
        return jnp.take(grouped, inverse, axis=0).reshape(total, columns.shape[1])

    gathered = (
        lax.all_to_all(b_gate[0], "unit", split_axis=1, concat_axis=0, tiled=True),
        lax.all_to_all(b_up[0], "unit", split_axis=1, concat_axis=0, tiled=True),
    )
    returned = (
        lax.all_to_all(relocate(gathered[0]), "unit", split_axis=0, concat_axis=1, tiled=True),
        lax.all_to_all(relocate(gathered[1]), "unit", split_axis=0, concat_axis=1, tiled=True),
    )
    merged_gate = average(a_gate[0], returned[0])
    merged_up = average(a_up[0], returned[1])
    dims = (((1,), (1,)), ((), ()))
    piece = lax.all_gather(calib, ("expert", "unit"), axis=0, tiled=True)
    gate_pre = lax.dot_general(merged_gate, piece, dims, preferred_element_type=jnp.float32)
    up_pre = lax.dot_general(merged_up, piece, dims, preferred_element_type=jnp.float32)
    hidden = (jax.nn.silu(gate_pre) * up_pre).astype(jnp.bfloat16)
    return (merged_gate[None], merged_up[None], hidden[None])


def solution(mesh):
    in_specs = (
        P("expert", "unit", None),
        P("expert", "unit", None),
        P("expert", "unit", None),
        P("expert", "unit", None),
        P("expert", None),
        P(("expert", "unit"), None),
    )
    out_specs = (P("expert", "unit", None), P("expert", "unit", None), P("expert", "unit", None))
    return jax.shard_map(local, mesh=mesh, in_specs=in_specs, out_specs=out_specs, check_vma=False)
```

profile of v0, /device:TPU:0, one launch (start us, length us, event | category | flops | bytes accessed | tf_op | source)
XLA Modules:
  0.0 1635.2 jit_solution(6001479759196739935)
XLA Ops:
  7.2 18.6 %copy.22 = bf16[1,1792,4096]{1,2,0:T(8,128)(2,1)} copy(bf16[1,1792,4096]{2,1,0:T(8,128)(2,1)} %param.10) | data formatting | bytes 29360128 | tf_op args[2]
  25.8 7.3 all-to-all-start
  33.1 18.6 %copy.26 = bf16[1,1792,4096]{1,2,0:T(8,128)(2,1)} copy(bf16[1,1792,4096]{2,1,0:T(8,128)(2,1)} %param.11) | data formatting | bytes 29360128 | tf_op args[3]
  51.7 299.4 %all-to-all-done = bf16[1792,8,512]{0,2,1:T(8,128)(2,1)} async-done(((bf16[1792,8,512]{0,2,1:T(8,128)(2,1)}), bf16[1792,8,512]{0,2,1:T(8,128)(2,1)}, u32[]{:S(2)}, u32[]{:S(2)}) %all-to-all-start) | async-done | bytes 14680096 | tf_op jit(solution)/shard_map/all_to_all | solution.py:23
  351.1 5.7 all-to-all-start.2
  356.8 2.9 scatter_custom_fusion
  359.8 18.7 %copy.23 = bf16[8,1792,512]{2,1,0:T(8,128)(2,1)} copy(bf16[8,1792,512]{1,2,0:T(8,128)(2,1)} %bitcast.3) | data formatting | bytes 29360128 | tf_op jit(solution)/shard_map/all_to_all | solution.py:23
  378.5 295.4 %all-to-all-done.2 = bf16[1792,8,512]{0,2,1:T(8,128)(2,1)} async-done(((bf16[1792,8,512]{0,2,1:T(8,128)(2,1)}), bf16[1792,8,512]{0,2,1:T(8,128)(2,1)}, u32[]{:S(2)}, u32[]{:S(2)}) %all-to-all-start.2) | async-done | bytes 14680096 | tf_op jit(solution)/shard_map/all_to_all | solution.py:24
  673.8 18.7 %copy.27 = bf16[8,1792,512]{2,1,0:T(8,128)(2,1)} copy(bf16[8,1792,512]{1,2,0:T(8,128)(2,1)} %bitcast.9) | data formatting | bytes 29360128 | tf_op jit(solution)/shard_map/all_to_all | solution.py:24
  692.5 18.6 %gather_fusion = bf16[448,32,512]{2,1,0:T(8,128)(2,1)} fusion(bf16[448,32,512]{2,1,0:T(8,128)(2,1)} %bitcast.50, s32[1024]{0:T(1024)S(1)} %pad_clamp_fusion), kind=kCustom, calls=%fused_computation.clone | custom fusion | bytes 29361920 | tf_op jit(solution)/shard_map/jit(_take)/gather | solution.py:20
  711.1 18.6 %gather_fusion.1 = bf16[448,32,512]{2,1,0:T(8,128)(2,1)} fusion(bf16[448,32,512]{2,1,0:T(8,128)(2,1)} %bitcast.52, s32[1024]{0:T(1024)S(1)} %pad_clamp_fusion), kind=kCustom, calls=%fused_computation.1.clone | custom fusion | bytes 29361920 | tf_op jit(solution)/shard_map/jit(_take)/gather | solution.py:20
  729.7 17.3 %broadcast_select_fusion = (bf16[448,32,512]{2,1,0:T(8,128)(2,1)S(1)}, bf16[448,32,512]{2,1,0:T(8,128)(2,1)}) fusion(bf16[448,32,512]{2,1,0:T(8,128)(2,1)} %gather_fusion.1, pred[448]{0:T(512)(128)(4,1)S(1)} %compare_and_fusion, bf16[448,32,512]{2,1,0:T(8,128)(2,1)} %gather_fusion), kind=kLoop, calls=%fused_computation.19 | loop fusion | flops 14680064 | bytes 58720704 | tf_op jit(solution)/shard_map/jit(_take)/select_n | solution.py:20
  747.0 321.5 %all_to_all.58 = bf16[8,1792,512]{2,1,0:T(8,128)(2,1)} all-to-all(bf16[8,1792,512]{2,1,0:T(8,128)(2,1)S(1)} %bitcast.51), channel_id=1, replica_groups=mesh['expert'=4,'unit'=8] {'unit'}, dimensions={0} | all-to-all | bytes 29360128 | tf_op jit(solution)/shard_map/all_to_all | solution.py:28
  1068.5 5.5 all-to-all-start.1
  1074.7 18.6 %copy.21 = bf16[1,1792,4096]{1,2,0:T(8,128)(2,1)} copy(bf16[1,1792,4096]{2,1,0:T(8,128)(2,1)} %param.8) | data formatting | bytes 29360128 | tf_op args[0]
  1093.4 18.8 %copy.25 = bf16[1,1792,4096]{1,2,0:T(8,128)(2,1)} copy(bf16[1,1792,4096]{2,1,0:T(8,128)(2,1)} %param.9) | data formatting | bytes 29360128 | tf_op args[1]
  1112.1 286.1 %all-gather.3.cloned.1.call-done = bf16[32,4,4096]{2,1,0:T(4,128)(2,1)} async-done(((bf16[1,4,4096]{2,1,0:T(4,128)(2,1)}), bf16[32,4,4096]{2,1,0:T(4,128)(2,1)}) %all-gather.3.cloned.1.call-update) | async-done | bytes 1048592 | tf_op jit(solution)/shard_map/all_gather | solution.py:33
  1398.2 1.3 reshape.132
  1399.5 16.8 %convert_bitcast_fusion.2 = f32[1792,8,512]{2,0,1:T(8,128)} fusion(bf16[8,1792,512]{2,1,0:T(8,128)(2,1)} %all_to_all.58), kind=kLoop, calls=%fused_computation.17 | loop fusion | flops 7340032 | bytes 44040192 | tf_op jit(solution)/shard_map/convert_element_type | solution.py:10
  1416.3 27.6 %copy.28 = f32[1792,8,512]{0,2,1:T(8,128)} copy(f32[1792,8,512]{2,0,1:T(8,128)} %convert_bitcast_fusion.2) | data formatting | bytes 58720256 | tf_op jit(solution)/shard_map/convert_element_type | solution.py:10
  1444.0 20.5 %fusion.9 = bf16[1792,4096]{0,1:T(8,128)(2,1)} fusion(bf16[1,1792,4096]{1,2,0:T(8,128)(2,1)} %copy.25, f32[1792,8,512]{0,2,1:T(8,128)} %copy.28), kind=kLoop, calls=%fused_computation.16 | loop fusion | flops 29360128 | bytes 58720256 | tf_op jit(solution)/shard_map/convert_element_type | solution.py:10
  1464.5 6.9 copy-done
  1471.4 14.6 fusion.6
  1486.0 16.8 %convert_bitcast_fusion.3 = f32[1792,8,512]{2,0,1:T(8,128)} fusion(bf16[8,1792,512]{2,1,0:T(8,128)(2,1)} %all-to-all-done.1), kind=kLoop, calls=%fused_computation.18 | loop fusion | flops 7340032 | bytes 44040192 | tf_op jit(solution)/shard_map/convert_element_type | solution.py:10
  1502.8 27.6 %copy.24 = f32[1792,8,512]{0,2,1:T(8,128)} copy(f32[1792,8,512]{2,0,1:T(8,128)} %convert_bitcast_fusion.3) | data formatting | bytes 58720256 | tf_op jit(solution)/shard_map/convert_element_type | solution.py:10
  1530.5 20.5 %fusion.4 = bf16[1792,4096]{0,1:T(8,128)(2,1)} fusion(bf16[1,1792,4096]{1,2,0:T(8,128)(2,1)} %copy.21, f32[1792,8,512]{0,2,1:T(8,128)} %copy.24), kind=kLoop, calls=%fused_computation.11 | loop fusion | flops 29360128 | bytes 58720256 | tf_op jit(solution)/shard_map/convert_element_type | solution.py:10
  1551.0 6.9 copy-done.1
  1557.9 14.6 fusion.1
  1572.5 20.1 %copy.32 = bf16[1,1792,4096]{2,1,0:T(8,128)(2,1)} copy(bf16[1,1792,4096]{1,2,0:T(8,128)(2,1)} %fusion.6) | data formatting | bytes 29360128
  1592.6 20.1 %copy.31 = bf16[1,1792,4096]{2,1,0:T(8,128)(2,1)} copy(bf16[1,1792,4096]{1,2,0:T(8,128)(2,1)} %fusion.1) | data formatting | bytes 29360128
  1612.7 7.3 fusion.14
  1620.0 8.3 fusion.11
  (12 shorter events, 0.8 us)
Async XLA Ops:
  25.8 325.3 %all-to-all-start = ((bf16[1792,8,512]{0,2,1:T(8,128)(2,1)}), bf16[1792,8,512]{0,2,1:T(8,128)(2,1)}, u32[]{:S(2)}, u32[]{:S(2)}) async-start(bf16[1792,8,512]{0,2,1:T(8,128)(2,1)} %bitcast.48), calls=%async_computation | async-start | bytes 29360128 | tf_op jit(solution)/shard_map/all_to_all | solution.py:23
  351.1 5.7 copy-start.2
  351.1 322.8 %all-to-all-start.2 = ((bf16[1792,8,512]{0,2,1:T(8,128)(2,1)}), bf16[1792,8,512]{0,2,1:T(8,128)(2,1)}, u32[]{:S(2)}, u32[]{:S(2)}) async-start(bf16[1792,8,512]{0,2,1:T(8,128)(2,1)} %bitcast.47), calls=%async_computation.2 | async-start | bytes 29360128 | tf_op jit(solution)/shard_map/all_to_all | solution.py:24
  1068.5 417.6 %all-to-all-start.1 = ((bf16[8,1792,512]{2,1,0:T(8,128)(2,1)}), bf16[8,1792,512]{2,1,0:T(8,128)(2,1)}, u32[]{:S(2)}, u32[]{:S(2)}) async-start(bf16[8,1792,512]{2,1,0:T(8,128)(2,1)} %bitcast.49), calls=%async_computation.1 | async-start | bytes 29360128 | tf_op jit(solution)/shard_map/all_to_all | solution.py:27
  1074.0 324.2 %all-gather.3.cloned.1.call-start = ((), (), s32[]{:S(2)}) async-start(), calls=%async_computation.4 | async-start | bytes 1081344 | tf_op jit(solution)/shard_map/all_gather | solution.py:33
  1444.0 27.5 %copy-start = (f32[1792,8,512]{0,2,1:T(8,128)S(1)}, f32[1792,8,512]{0,2,1:T(8,128)}, u32[]{:S(2)}) copy-start(f32[1792,8,512]{0,2,1:T(8,128)} %copy.28) | copy-start | bytes 88080384
  1530.5 27.5 %copy-start.1 = (f32[1792,8,512]{0,2,1:T(8,128)S(1)}, f32[1792,8,512]{0,2,1:T(8,128)}, u32[]{:S(2)}) copy-start(f32[1792,8,512]{0,2,1:T(8,128)} %copy.24) | copy-start | bytes 88080384
Sparse Core Ops, SparseCore 0:
  1077.8 320.3 all-gather.2
where the time goes:
time: 1640 us
  waiting for transfers between devices  881 us (54%)
  blocking collectives  322 us (20%)
  local copies, waits for them, and re-layouts  263 us (16%)
  other arithmetic  121 us (7%)
  starting transfers between devices  18.7 us (1%)
    all_to_all x1, blocking collectives, local(): lax.all_to_all(relocate(gathered[1]), 'unit', split_axis=0, concat_axis=1...  322 us
    all_to_all x1, waiting for transfers between devices, local(): lax.all_to_all(b_gate[0], 'unit', split_axis=1, concat_axis=0, tiled=True)  299 us
    all_to_all x1, waiting for transfers between devices, local(): lax.all_to_all(b_up[0], 'unit', split_axis=1, concat_axis=0, tiled=True)  295 us
    all_gather x1, waiting for transfers between devices, local(): piece = lax.all_gather(calib, ('expert', 'unit'), axis=0, tiled=True)  286 us
    unnamed x13, local copies, waits for them, and re-layouts  130 us
    convert_element_type x4, other arithmetic, average(): ((first.astype(jnp.float32) + second.astype(jnp.float32)) * 0.5).astype(j...  70.3 us
    convert_element_type x2, local copies, waits for them, and re-layouts, average(): second.astype(jnp.float32)  55.3 us
    gather x2, local copies, waits for them, and re-layouts, relocate(): return jnp.take(grouped, inverse, axis=0).reshape(total, columns.shape[1])  37.1 us
  transfers between devices with their start and end apart: 4, of which 3 were waited for; matrix products, arithmetic and copies ran while one was open for 10% of the time, Pallas kernels for 0%

commit v1 on v0

v1 whole, which is shorter than its diff:
```python
import functools

import jax
import jax.numpy as jnp
from jax import lax
from jax.experimental import pallas as pl
from jax.experimental.pallas import tpu as pltpu
from jax.sharding import PartitionSpec as P

BLOCK = 32


def merge_kernel(ways, a_ref, r_ref, calib_ref, m_ref, pre_ref):
    wide = a_ref.shape[1] // ways
    total = None
    for way in range(ways):
        columns = slice(way * wide, (way + 1) * wide)
        merged = (
            (a_ref[:, columns].astype(jnp.float32) + r_ref[way].astype(jnp.float32)) * 0.5
        ).astype(jnp.bfloat16)
        m_ref[:, columns] = merged
        term = lax.dot_general(
            merged, calib_ref[:, columns], (((1,), (1,)), ((), ())), preferred_element_type=jnp.float32
        )
        total = term if total is None else total + term
    pre_ref[...] = total


def merge_xla(a, returned, calib):
    rows, width = a.shape
    returned = jnp.swapaxes(returned, 0, 1).reshape(rows, width)
    merged = ((a.astype(jnp.float32) + returned.astype(jnp.float32)) * 0.5).astype(jnp.bfloat16)
    pre = lax.dot_general(merged, calib, (((1,), (1,)), ((), ())), preferred_element_type=jnp.float32)
    return merged, pre


def merge(a, returned, calib):
    ways, rows, wide = returned.shape
    tokens, width = calib.shape
    if wide % 128:
        return merge_xla(a, returned, calib)
    tile = next(t for t in (256, 224, 128, 64, 32) if rows % t == 0)
    return pl.pallas_call(
        functools.partial(merge_kernel, ways),
        grid=(rows // tile,),
        in_specs=[
            pl.BlockSpec((tile, width), lambda i: (i, 0)),
            pl.BlockSpec((ways, tile, wide), lambda i: (0, i, 0)),
            pl.BlockSpec((tokens, width), lambda i: (0, 0)),
        ],
        out_specs=[
            pl.BlockSpec((tile, width), lambda i: (i, 0)),
            pl.BlockSpec((tile, tokens), lambda i: (i, 0)),
        ],
        out_shape=[
            jax.ShapeDtypeStruct((rows, width), jnp.bfloat16),
            jax.ShapeDtypeStruct((rows, tokens), jnp.float32),
        ],
        compiler_params=pltpu.CompilerParams(vmem_limit_bytes=40 * 1024 * 1024),
        cost_estimate=pl.CostEstimate(
            flops=2 * rows * width * tokens, bytes_accessed=6 * rows * width, transcendentals=0
        ),
    )(a, returned, calib)


def local(a_gate, a_up, b_gate, b_up, order, calib):
    blocks = order.shape[1]
    ways = lax.axis_size("unit")
    inverse = jnp.zeros((blocks,), jnp.int32).at[order[0]].set(jnp.arange(blocks, dtype=jnp.int32))
    everyone = lax.all_gather(calib, ("expert", "unit"), axis=0, tiled=True)

    def columns_of(b):
        rows, width = b.shape
        return jnp.swapaxes(b.reshape(rows, ways, width // ways), 0, 1)

    def relocate(columns):
        _, rows, wide = columns.shape
        grouped = columns.reshape(blocks, BLOCK, wide)
        return jnp.take(grouped, inverse, axis=0, mode="clip").reshape(ways, rows, wide)

    def bring(columns):
        return lax.all_to_all(columns, "unit", split_axis=0, concat_axis=0, tiled=True)

    gate = bring(columns_of(b_gate[0]))
    up_columns, everyone = lax.optimization_barrier((columns_of(b_up[0]), everyone))
    up = bring(up_columns)
    gate = bring(relocate(gate))
    up = bring(relocate(up))
    merged_gate, gate_pre = merge(a_gate[0], gate, everyone)
    merged_up, up_pre = merge(a_up[0], up, everyone)
    hidden = (jax.nn.silu(gate_pre) * up_pre).astype(jnp.bfloat16)
    return (merged_gate[None], merged_up[None], hidden[None])


def solution(mesh):
    in_specs = (
        P("expert", "unit", None),
        P("expert", "unit", None),
        P("expert", "unit", None),
        P("expert", "unit", None),
        P("expert", None),
        P(("expert", "unit"), None),
    )
    out_specs = (P("expert", "unit", None), P("expert", "unit", None), P("expert", "unit", None))
    return jax.shard_map(local, mesh=mesh, in_specs=in_specs, out_specs=out_specs, check_vma=False)
```

time: 1640 us -> 1360 us (0.83)
  blocking collectives: 322 us -> 0 us
  waiting for transfers between devices: 881 us -> 1160 us
  local copies, waits for them, and re-layouts: 263 us -> 116 us
  other arithmetic: 121 us -> 1.03 us
  Pallas kernels: 0 us -> 36 us
    all_to_all x1 -> x0, blocking collectives: 322 us -> none  [local(): lax.all_to_all(relocate(gathered[1]), 'unit', split_axis=0, concat_axis=1...]
    all_to_all x3 -> x4, waiting for transfers between devices: 595 us -> 858 us  [bring(): lax.all_to_all(columns, 'unit', split_axis=0, concat_axis=0, tiled=True)]
    convert_element_type x6 -> x0, other arithmetic: 104 us -> none  [the longest x4 70.3 us: average(): ((first.astype(jnp.float32) + second.astype(jnp.float32)) * 0.5).astype(j...]
    unnamed x13 -> x4, local copies, waits for them, and re-layouts: 130 us -> 37.4 us
    convert_element_type x2 -> x0, local copies, waits for them, and re-layouts: 55.3 us -> none  [average(): second.astype(jnp.float32)]
    pallas_call x0 -> x2, Pallas kernels: none -> 36 us  [merge(): pl.pallas_call(functools.partial(merge_kernel, ways), grid=(rows // tile,...]
    all_gather x1, waiting for transfers between devices: 286 us -> 306 us  [local(): everyone = lax.all_gather(calib, ('expert', 'unit'), axis=0, tiled=True)]
    select_n x2 -> x0, other arithmetic: 17.3 us -> none  [relocate(): return jnp.take(grouped, inverse, axis=0).reshape(total, columns.shape[1])]
  transfers between devices with their start and end apart: 4 -> 5, of which waited for: 3 -> 4; matrix products, arithmetic and copies ran while one was open for 10% -> 7% of each run, Pallas kernels for 0% -> 1%
where the time goes in v1:
time: 1360 us
  waiting for transfers between devices  1160 us (85%)
  local copies, waits for them, and re-layouts  116 us (9%)
  Pallas kernels  36 us (3%)
  starting transfers between devices  24 us (2%)
  between operations  14.1 us (1%)
    all_to_all x4, waiting for transfers between devices, bring(): lax.all_to_all(columns, 'unit', split_axis=0, concat_axis=0, tiled=True)  858 us
    all_gather x1, waiting for transfers between devices, local(): everyone = lax.all_gather(calib, ('expert', 'unit'), axis=0, tiled=True)  306 us
    unnamed x4, local copies, waits for them, and re-layouts  37.4 us
    all_to_all x2, local copies, waits for them, and re-layouts, bring(): lax.all_to_all(columns, 'unit', split_axis=0, concat_axis=0, tiled=True)  37.4 us
    gather x2, local copies, waits for them, and re-layouts, relocate(): jnp.take(grouped, inverse, axis=0, mode='clip').reshape(ways, rows, wide)  37.1 us
    pallas_call x2, Pallas kernels, merge(): pl.pallas_call(functools.partial(merge_kernel, ways), grid=(rows // tile,...  36 us
  transfers between devices with their start and end apart: 5, of which 4 were waited for; matrix products, arithmetic and copies ran while one was open for 7% of the time, Pallas kernels for 1%

profile of v1, /device:TPU:0, one launch (start us, length us, event | category | flops | bytes accessed | tf_op | source)
XLA Modules:
  0.0 1355.4 jit_solution(16118191173897559573)
XLA Ops:
  7.2 18.6 %copy.13 = bf16[1,1792,4096]{1,2,0:T(8,128)(2,1)} copy(bf16[1,1792,4096]{2,1,0:T(8,128)(2,1)} %param.8) | data formatting | bytes 29360128 | tf_op args[2]
  25.8 7.3 all-to-all-start
  33.1 0.0 all-gather.3.cloned.1.call-start
  33.1 0.7 all-gather.3.cloned.1.call-update
  33.8 18.8 %copy.15 = bf16[1,1792,4096]{1,2,0:T(8,128)(2,1)} copy(bf16[1,1792,4096]{2,1,0:T(8,128)(2,1)} %param.9) | data formatting | bytes 29360128 | tf_op args[3]
  52.6 305.7 %all-gather.3.cloned.1.call-done = bf16[32,4,4096]{2,1,0:T(4,128)(2,1)} async-done(((bf16[1,4,4096]{2,1,0:T(4,128)(2,1)}), bf16[32,4,4096]{2,1,0:T(4,128)(2,1)}) %all-gather.3.cloned.1.call-update) | async-done | bytes 1048592 | tf_op jit(solution)/shard_map/all_gather | solution.py:70
  358.3 1.3 reshape.77.calib_ref
  359.6 0.0 copy-start
  359.7 0.0 all-to-all-done
  359.7 5.6 all-to-all-start.2
  365.2 0.0 copy-done
  365.3 2.9 scatter_custom_fusion
  368.2 18.7 %copy.14 = bf16[8,1792,512]{2,1,0:T(8,128)(2,1)} copy(bf16[8,1792,512]{1,2,0:T(8,128)(2,1)} %all-to-all-done) | data formatting | bytes 29360128 | tf_op jit(solution)/shard_map/all_to_all | solution.py:82
  386.9 18.6 %gather_fusion = bf16[448,32,512]{2,1,0:T(8,128)(2,1)} fusion(bf16[448,32,512]{2,1,0:T(8,128)(2,1)} %bitcast.26, s32[1024]{0:T(1024)S(1)} %pad_clamp_fusion), kind=kCustom, calls=%fused_computation | custom fusion | bytes 29361920 | tf_op jit(solution)/shard_map/jit(_take)/gather | solution.py:79
  405.5 278.3 %all-to-all-done.2 = bf16[8,1792,512]{1,2,0:T(8,128)(2,1)} async-done(((bf16[8,1792,512]{1,2,0:T(8,128)(2,1)}), bf16[8,1792,512]{1,2,0:T(8,128)(2,1)}, u32[]{:S(2)}, u32[]{:S(2)}) %all-to-all-start.2) | async-done | bytes 14680096 | tf_op jit(solution)/shard_map/all_to_all | solution.py:82
  683.8 5.5 all-to-all-start.1
  689.4 18.7 %copy.16 = bf16[8,1792,512]{2,1,0:T(8,128)(2,1)} copy(bf16[8,1792,512]{1,2,0:T(8,128)(2,1)} %all-to-all-done.2) | data formatting | bytes 29360128 | tf_op jit(solution)/shard_map/all_to_all | solution.py:82
  708.1 18.5 %gather_fusion.1 = bf16[448,32,512]{2,1,0:T(8,128)(2,1)} fusion(bf16[448,32,512]{2,1,0:T(8,128)(2,1)} %bitcast.25, s32[1024]{0:T(1024)S(1)} %pad_clamp_fusion), kind=kCustom, calls=%fused_computation.1 | custom fusion | bytes 29361920 | tf_op jit(solution)/shard_map/jit(_take)/gather | solution.py:79
  726.6 280.5 %all-to-all-done.1.r_ref = bf16[8,1792,512]{2,1,0:T(8,128)(2,1)} async-done(((bf16[8,1792,512]{2,1,0:T(8,128)(2,1)}), bf16[8,1792,512]{2,1,0:T(8,128)(2,1)}, u32[]{:S(2)}, u32[]{:S(2)}) %all-to-all-start.1) | async-done | bytes 14680096 | tf_op jit(solution)/shard_map/all_to_all | solution.py:82
  1007.0 5.6 all-to-all-start.3
  1012.6 18.0 %shard_map.85 = (bf16[1792,4096]{1,0:T(8,128)(2,1)}, f32[1792,128]{1,0:T(8,128)S(1)}) custom-call(bf16[1792,4096]{1,0:T(8,128)(2,1)} %bitcast.27, bf16[8,1792,512]{2,1,0:T(8,128)(2,1)} %all-to-all-done.1.r_ref, bf16[128,4096]{1,0:T(8,128)(2,1)S(1)} %reshape.77.calib_ref), custom_call_target="tpu_custom_call" | custom-call | flops 1879048192 | bytes 44040192 | tf_op jit(solution)/shard_map/pallas_call | solution.py:43
  1030.6 298.9 %all-to-all-done.3.r_ref = bf16[8,1792,512]{2,1,0:T(8,128)(2,1)} async-done(((bf16[8,1792,512]{2,1,0:T(8,128)(2,1)}), bf16[8,1792,512]{2,1,0:T(8,128)(2,1)}, u32[]{:S(2)}, u32[]{:S(2)}) %all-to-all-start.3) | async-done | bytes 14680096 | tf_op jit(solution)/shard_map/all_to_all | solution.py:82
  1329.5 18.0 %shard_map.86 = (bf16[1792,4096]{1,0:T(8,128)(2,1)}, f32[1792,128]{1,0:T(8,128)S(1)}) custom-call(bf16[1792,4096]{1,0:T(8,128)(2,1)} %bitcast.28, bf16[8,1792,512]{2,1,0:T(8,128)(2,1)} %all-to-all-done.3.r_ref, bf16[128,4096]{1,0:T(8,128)(2,1)S(1)} %reshape.77.calib_ref), custom_call_target="tpu_custom_call" | custom-call | flops 1879048192 | bytes 44040192 | tf_op jit(solution)/shard_map/pallas_call | solution.py:43
  1347.5 1.0 fusion
  (3 shorter events, 0.0 us)
Async XLA Ops:
  25.8 333.9 %all-to-all-start = ((bf16[8,1792,512]{1,2,0:T(8,128)(2,1)}), bf16[8,1792,512]{1,2,0:T(8,128)(2,1)}, u32[]{:S(2)}, u32[]{:S(2)}) async-start(bf16[8,1792,512]{1,2,0:T(8,128)(2,1)} %bitcast.22), calls=%async_computation | async-start | bytes 29360128 | tf_op jit(solution)/shard_map/all_to_all | solution.py:82
  33.1 325.2 %all-gather.3.cloned.1.call-start = ((), (), s32[]{:S(2)}) async-start(), calls=%async_computation.4 | async-start | bytes 1081344 | tf_op jit(solution)/shard_map/all_gather | solution.py:70
  359.6 5.6 copy-start
  359.7 324.1 %all-to-all-start.2 = ((bf16[8,1792,512]{1,2,0:T(8,128)(2,1)}), bf16[8,1792,512]{1,2,0:T(8,128)(2,1)}, u32[]{:S(2)}, u32[]{:S(2)}) async-start(bf16[8,1792,512]{1,2,0:T(8,128)(2,1)} %bitcast.21), calls=%async_computation.2 | async-start | bytes 29360128 | tf_op jit(solution)/shard_map/all_to_all | solution.py:82
  683.8 323.2 %all-to-all-start.1 = ((bf16[8,1792,512]{2,1,0:T(8,128)(2,1)}), bf16[8,1792,512]{2,1,0:T(8,128)(2,1)}, u32[]{:S(2)}, u32[]{:S(2)}) async-start(bf16[8,1792,512]{2,1,0:T(8,128)(2,1)} %bitcast.23), calls=%async_computation.1 | async-start | bytes 29360128 | tf_op jit(solution)/shard_map/all_to_all | solution.py:82
  1007.0 322.5 %all-to-all-start.3 = ((bf16[8,1792,512]{2,1,0:T(8,128)(2,1)}), bf16[8,1792,512]{2,1,0:T(8,128)(2,1)}, u32[]{:S(2)}, u32[]{:S(2)}) async-start(bf16[8,1792,512]{2,1,0:T(8,128)(2,1)} %bitcast.24), calls=%async_computation.3 | async-start | bytes 29360128 | tf_op jit(solution)/shard_map/all_to_all | solution.py:82
Sparse Core Ops, SparseCore 0:
  36.9 321.3 all-gather.2
